TPU v7x, 32 devices: a whole 2x2x4 slice. The times are simulated.
32 devices in a mesh: groups: 2 (over x), row: 8 (over z, y), col: 2 (over core).
Axes of the slice: x: 2, y: 2, z: 4, core: 2. Of those that a mesh axis runs over, the one named last changes fastest.
Arguments:
- inverse: float32 [16, 2, 128, 2048], P('groups', 'col', None, 'row'), parts along dimension 0, as said below
- features: float32 [16384, 1024], P(('groups', 'row')), parts along dimension 0, may hold values from -6 to 6
- residual: float32 [16384, 256], P(('groups', 'row')), parts along dimension 0, may hold values from -6 to 6
- block_ids: int32 [4096], P(('groups', 'row')), parts along dimension 0, may hold values from 0 to 8191, as said below
Outputs:
- updated: float32 [16384, 256], P(('groups', 'row'), 'col'), parts along dimension 0
There are 2 independent parts, one for each index of `groups`. A program takes and returns all parts, laid end to end along the dimension named above; each array names one. Nothing has to cross between parts.
Inputs may be any that keep to these rules, and one draw needn't show every extreme that they name: `block_ids`: the ids at block positions a * 256 to (a + 1) * 256 - 1 are distinct and lie in a * 1024 to (a + 1) * 1024 - 1. `inverse`: read as a [2048, 2048] matrix, each row is a positive scale between 0.3 and 3.4 times an identity row plus small independent entries.
All inputs are finite; a program needn't handle non-finite values.
Results may differ from a plain program's by a relative error of at most 0.000084.
Values sent between devices are 32-bit elements; how exact they have to be, the bound alone decides.
A program may use at most 128 MiB of HBM per device.

v0:
```python
import functools

import jax
import jax.numpy as jnp
from jax import lax
from jax.experimental import pallas as pl
from jax.experimental.pallas import tpu as pltpu
from jax.sharding import PartitionSpec as P

F32, BF16 = jnp.float32, jnp.bfloat16
MESH = pl.DeviceIdType.MESH
NN = (((1,), (0,)), ((), ()))
NT = (((1,), (1,)), ((), ()))


def split(v):
    hi = v.astype(BF16)
    return hi, (v - hi.astype(F32)).astype(BF16)


def dot3(a, b, dims):
    def one(x, y):
        return lax.dot_general(x, y, dims, preferred_element_type=F32)

    return one(a[0], b[1]) + one(a[1], b[0]) + one(a[0], b[0])


def kernel(
    n, snake, ids, feat_hbm, res_hbm, inv_hbm, out, feat, fhi, flo, res, inv, bres, xh, xl, xbuf,
    kbuf, cbuf, rbuf, change, ebuf, lsem, xs_sem, xr_sem, ss_sem, sr_sem, es_sem, er_sem,
):
    me, core = lax.axis_index("row"), lax.axis_index("col")
    half_n = n // 2
    rows, feats = feat.shape
    blk = ids.shape[0]
    half = blk // 2
    quarter = half // 2
    width = out.shape[1]
    slots = kbuf.shape[0]
    tile = min(512, rows)

    def pos_of(r):
        if not snake:
            return r
        z, y = r // 2, r % 2
        return (1 - y) * z + y * (n - 1 - z)

    def row_of(p):
        p = lax.rem(p + n, n)
        if not snake:
            return p
        q = p // half_n
        return (1 - q) * 2 * p + q * (2 * (n - 1 - p) + 1)

    pos = pos_of(me)
    ahead = (row_of(pos + 1), row_of(pos + n - 1))
    sign = (1, -1)

    loads = [
        pltpu.make_async_copy(feat_hbm, feat, lsem.at[0]),
        pltpu.make_async_copy(res_hbm, res, lsem.at[1]),
        pltpu.make_async_copy(inv_hbm, inv, lsem.at[2]),
    ]
    for load in loads:
        load.start()
    barrier = pltpu.get_barrier_semaphore()
    for target in ({"row": ahead[0]}, {"row": ahead[1]}, {"col": 1 - core}):
        pl.semaphore_signal(barrier, inc=1, device_id=target, device_id_type=MESH)

    def remote(src, dst, send, recv, target):
        return pltpu.make_async_remote_copy(
            src_ref=src, dst_ref=dst, send_sem=send, recv_sem=recv, device_id=target,
            device_id_type=MESH,
        )

    def x_copy(way, p):
        d, h = p // 2 + 1, (p + way) % 2
        src = way * half + h * quarter
        dst = way * quarter if d == half_n else src
        return remote(
            xbuf.at[d - 1, pl.ds(src, quarter)], xbuf.at[d, pl.ds(dst, quarter)],
            xs_sem.at[way, p], xr_sem.at[way, p], {"row": ahead[way]},
        )

    def small_copy(way, m):
        if m <= half_n:
            at = pl.ds(way * quarter, quarter) if m == 1 else pl.ds(0, half)
            src, dst = rbuf.at[way, m - 1, at], rbuf.at[way, m, at]
        else:
            s = m - half_n
            if s == half_n:
                src = cbuf.at[s - 1, pl.ds(way * half + way * quarter, quarter)]
                dst = cbuf.at[s, pl.ds(way * quarter, quarter)]
            else:
                src = cbuf.at[s - 1, pl.ds(way * half, half)]
                dst = cbuf.at[s, pl.ds(way * half, half)]
        return remote(
            src, dst, ss_sem.at[way, m - 1], sr_sem.at[way, m - 1], {"row": ahead[way]}
        )

    def partial_value(owner, at=None):
        a = inv[owner, 0] if at is None else inv[owner, 0, at]
        return dot3(split(a), (bres[0], bres[1]), NN)

    def gram(d, cols):
        hi, lo = split(xbuf[d, pl.ds(0, cols)])
        xh[pl.ds(0, cols)] = hi
        xl[pl.ds(0, cols)] = lo

        def body(i, _):
            at = pl.ds(pl.multiple_of(i * tile, tile), tile)
            g = dot3((fhi[at], flo[at]), (xh[pl.ds(0, cols)], xl[pl.ds(0, cols)]), NT)
            g = g * (1.0 / feats) + 0.5
            kbuf[d % slots, at, pl.ds(0, cols)] = g * g
            return 0

        lax.fori_loop(0, rows // tile, body, 0)

    def apply(d, cols):
        c = split(cbuf[d, pl.ds(0, cols)])

        def body(i, _):
            at = pl.ds(pl.multiple_of(i * tile, tile), tile)
            add = dot3(split(kbuf[d % slots, at, pl.ds(0, cols)]), c, NN)
            change[at] = add if d == 0 else change[at] + add
            return 0

        lax.fori_loop(0, rows // tile, body, 0)

    base = me * rows

    def local(i):
        return jnp.maximum(jnp.minimum(ids[i] - base, rows - 1), 0)

    loads[0].wait()

    def gather_x(i, _):
        v = feat[pl.ds(local(core * half + i), 1), :]
        xbuf[0, pl.ds(i, 1), :] = v
        xbuf[0, pl.ds(half + i, 1), :] = v
        return 0

    lax.fori_loop(0, half, gather_x, 0, unroll=8)
    pl.semaphore_wait(barrier, 3)
    for way in (0, 1):
        x_copy(way, 0).start()

    loads[1].wait()

    def gather_res(i, _):
        change[pl.ds(i, 1), :] = res[pl.ds(local(i), 1), :]
        return 0

    lax.fori_loop(0, blk, gather_res, 0, unroll=8)
    hi, lo = split(change[pl.ds(0, blk)])
    bres[0] = hi
    bres[1] = lo
    loads[2].wait()
    for way in (0, 1):
        at = pl.ds(way * quarter, quarter)
        rbuf[way, 0, at] = partial_value(row_of(pos + half_n), at)
        small_copy(way, 1).start()

    def split_feat(i, _):
        at = pl.ds(pl.multiple_of(i * quarter, quarter), quarter)
        hi, lo = split(feat[at])
        fhi[at] = hi
        flo[at] = lo
        return 0

    lax.fori_loop(0, rows // quarter, split_feat, 0)
    for k in range(n):
        m = k + 1
        for way in (0, 1):
            small_copy(way, m).wait_recv()
            if m < half_n:
                part = partial_value(row_of(pos + n + sign[way] * (half_n - m)))
                if m == 1:
                    got, other = pl.ds(way * quarter, quarter), (1 - way) * quarter
                    lo_part, hi_part = part[:quarter], part[quarter:]
                    mine, rest = (lo_part, hi_part) if way == 0 else (hi_part, lo_part)
                    rbuf[way, 1, got] = rbuf[way, 1, got] + mine
                    rbuf[way, 1, pl.ds(other, quarter)] = rest
                else:
                    rbuf[way, m] = rbuf[way, m] + part
            elif m == half_n and way == 1:
                corr = partial_value(me) + rbuf[0, half_n] + rbuf[1, half_n]
                cbuf[0, pl.ds(0, half)] = corr
                cbuf[0, pl.ds(half, half)] = corr
                small_copy(0, m + 1).start()
            if m < n and (m != half_n or way == 1):
                small_copy(way, m + 1).start()
            if k >= 1:
                x_copy(way, k - 1).wait_recv()
            if k + 1 <= n - 2:
                x_copy(way, k + 1).start()
        if k == 0:
            gram(0, half)
        if k % 2 == 0 and k >= 2:
            gram(k // 2, blk)
        if k == half_n - 1:
            apply(0, half)
        if half_n <= k < n - 1:
            apply(k - half_n + 1, blk)

    gram(half_n, half)
    c = split(cbuf[half_n, pl.ds(0, half)])
    mine = pl.ds(pl.multiple_of(core * width, width), width)
    theirs = pl.ds(pl.multiple_of((1 - core) * width, width), width)
    step = tile // 2

    def swap(i):
        at = pl.ds(i * step, step)
        return remote(
            change.at[at, theirs], ebuf.at[at, pl.ds(0, width)], es_sem.at[i], er_sem.at[i],
            {"col": 1 - core},
        )

    for i in range(rows // step):
        at = pl.ds(i * step, step)
        change[at] += dot3(split(kbuf[half_n % slots, at, pl.ds(0, half)]), c, NN)
        swap(i).start()
    for i in range(rows // step):
        at = pl.ds(i * step, step)
        swap(i).wait_recv()
        out[at] = res[at, mine] - (change[at, mine] + ebuf[at, pl.ds(0, width)])
    for way in (0, 1):
        for p in range(n - 1):
            x_copy(way, p).wait_send()
        for m in range(1, n + 1):
            small_copy(way, m).wait_send()
    for i in range(rows // step):
        swap(i).wait_send()


def on_device(snake, inverse, features, residual, block_ids):
    n, cores = lax.axis_size("row"), lax.axis_size("col")
    rows, feats = features.shape
    rhs = residual.shape[1]
    blk = block_ids.shape[0]
    half, half_n = blk // cores, n // 2
    any_spec = pl.BlockSpec(memory_space=pl.ANY)
    dma = pltpu.SemaphoreType.DMA
    tiles = rows // (min(512, rows) // 2)
    return pl.pallas_call(
        functools.partial(kernel, n, snake),
        out_shape=jax.ShapeDtypeStruct((rows, rhs // cores), F32),
        in_specs=[pl.BlockSpec(memory_space=pltpu.SMEM), any_spec, any_spec, any_spec],
        out_specs=pl.BlockSpec(memory_space=pltpu.VMEM),
        scratch_shapes=[
            pltpu.VMEM((rows, feats), F32),
            pltpu.VMEM((rows, feats), BF16),
            pltpu.VMEM((rows, feats), BF16),
            pltpu.VMEM((rows, rhs), F32),
            pltpu.VMEM(inverse.shape, F32),
            pltpu.VMEM((2, blk, rhs), BF16),
            pltpu.VMEM((blk, feats), BF16),
            pltpu.VMEM((blk, feats), BF16),
            pltpu.VMEM((half_n + 1, blk, feats), F32),
            pltpu.VMEM((n // 4 + 2, rows, blk), F32),
            pltpu.VMEM((half_n + 1, blk, rhs), F32),
            pltpu.VMEM((2, half_n + 1, half, rhs), F32),
            pltpu.VMEM((rows, rhs), F32),
            pltpu.VMEM((rows, rhs), F32),
            dma((3,)),
            dma((2, n - 1)),
            dma((2, n - 1)),
            dma((2, n)),
            dma((2, n)),
            dma((tiles,)),
            dma((tiles,)),
        ],
        compiler_params=pltpu.CompilerParams(
            collective_id=0, has_side_effects=True, vmem_limit_bytes=67043328
        ),
    )(block_ids, features, residual, inverse)


def two_lines(mesh):
    line = mesh.devices
    line = line[0, :, 0] if line.ndim == 3 else line.ravel()
    places = [getattr(d, "coords", None) for d in line]
    if any(p is None for p in places):
        return True
    return len({tuple(p)[:2] for p in places}) == 2


def solution(mesh):
    return jax.shard_map(
        functools.partial(on_device, two_lines(mesh)),
        mesh=mesh,
        in_specs=(
            P("groups", "col", None, "row"),
            P(("groups", "row"), None),
            P(("groups", "row"), None),
            P(("groups", "row")),
        ),
        out_specs=P(("groups", "row"), "col"),
        check_vma=False,
    )
```

profile of v0, /device:TPU:1, one launch (start us, length us, event | category | flops | bytes accessed | tf_op | source)
XLA Modules:
  0.0 77.2 jit_solution(18436333157594248996)
XLA Ops:
  0.0 75.3 %shard_map.46 = f32[1024,128]{1,0:T(8,128)} custom-call(s32[256]{0:T(256)} %ids.1, f32[1024,1024]{1,0:T(8,128)} %feat_hbm.1, f32[1024,256]{1,0:T(8,128)} %res_hbm.1, f32[8,1,128,256]{3,2,1,0:T(8,128)} %inv_hbm.1), custom_call_target="tpu_custom_call" | custom-call | tf_op jit(solution)/shard_map/pallas_call | solution.py:245
  75.3 1.9 %copy.6 = f32[1024,128]{1,0:T(8,128)} copy(f32[1024,128]{1,0:T(8,128)} %shard_map.46) | data formatting | bytes 1048576
where the time goes:
time: 77.4 us; the launch traced here: 77.2 us
  Pallas kernels  75.3 us (97%)
  local copies, waits for them, and re-layouts  1.87 us (2%)
    pallas_call x1, Pallas kernels, on_device(): pl.pallas_call(functools.partial(kernel, n, snake), out_shape=jax.ShapeDt...  75.3 us
    unnamed x1, local copies, waits for them, and re-layouts  1.87 us

commit v1 on v0

--- a/solution.py
+++ b/solution.py
@@ -25,7 +25,7 @@
     return one(a[0], b[1]) + one(a[1], b[0]) + one(a[0], b[0])
 
 
-def kernel(
+def ring_kernel(
     n, snake, ids, feat_hbm, res_hbm, inv_hbm, out, feat, fhi, flo, res, inv, bres, xh, xl, xbuf,
     kbuf, cbuf, rbuf, change, ebuf, lsem, xs_sem, xr_sem, ss_sem, sr_sem, es_sem, er_sem,
 ):
@@ -233,7 +233,7 @@
         swap(i).wait_send()
 
 
-def on_device(snake, inverse, features, residual, block_ids):
+def ring(snake, inverse, features, residual, block_ids):
     n, cores = lax.axis_size("row"), lax.axis_size("col")
     rows, feats = features.shape
     rhs = residual.shape[1]
@@ -243,7 +243,7 @@
     dma = pltpu.SemaphoreType.DMA
     tiles = rows // (min(512, rows) // 2)
     return pl.pallas_call(
-        functools.partial(kernel, n, snake),
+        functools.partial(ring_kernel, n, snake),
         out_shape=jax.ShapeDtypeStruct((rows, rhs // cores), F32),
         in_specs=[pl.BlockSpec(memory_space=pltpu.SMEM), any_spec, any_spec, any_spec],
         out_specs=pl.BlockSpec(memory_space=pltpu.VMEM),
@@ -276,6 +276,361 @@
     )(block_ids, features, residual, inverse)
 
 
+CORNER_Z = (
+    "Xa0", "Xa1", "Rf", "Rd", "Rh", "Rb", "Xa2", "Xa3", "Rg", "Re", "Ra", "Rc",
+    "Xb0", "Xb1", "Xb2", "Xb3",
+)
+CORNER_Y = (
+    "Xa0", "Xa2", "Xa3", "Xa1", "Xc0", "Xc1", "Xc2", "Xc3", "Xe0", "Xg0", "Xe1", "Xg1",
+    "Xg2", "Xg3", "Xe2", "Xe3", "Cg", "Ce",
+)
+INNER_Z = (
+    "Xc0", "Xc1", "Xc2", "Xc3", "Xe2", "Xe3", "Xe0", "Xg0", "Xe1", "Xg1", "Xg2", "Xg3",
+    "Ca", "Cc", "Cg", "Ce", "Cb", "Cd",
+)
+INNER_W = (
+    "Xc0", "Xc2", "Xc3", "Xc1", "Sf", "Xa0", "Sh", "Xa1", "Xa2", "Xa3", "Sg", "Se", "Ca", "Cc",
+)
+INNER_Y = (
+    "Xc0", "Xc1", "Xc2", "Xe2", "Xe3", "Xc3", "Td", "Xg0", "Tb", "Xg1", "Xg2", "Xg3",
+    "Ca", "Cc", "Xe0", "Xe1", "Cg", "Ce",
+)
+OVER_Y = dict(zip("abcdefgh", "badcfehg"))
+OVER_Z = dict(zip("abcdefgh", "ghefcdab"))
+
+
+def seen(order, swap):
+    return [i[0] + swap.get(i[1], i[1]) + i[2:] for i in order]
+
+
+def slots(*links):
+    most = max(len(link) for link in links)
+    return [[link[k] for link in links if k < len(link)] for k in range(most)]
+
+
+def mesh_kernel(
+    ids, feat_hbm, res_hbm, inv_hbm, out, feat, fhi, flo, res, inv, bres, xall, xh, xl, khi, klo,
+    call, chi, clo, own, part, half_sum, col_sum, change, ebuf, lsem, xs, xr, cs, cr, rs, rr, ss,
+    sr, ts, tr, es, er,
+):
+    me, core = lax.axis_index("row"), lax.axis_index("col")
+    rows, feats = feat.shape
+    blk = ids.shape[0]
+    half = blk // 2
+    quarter = half // 4
+    width = out.shape[1]
+    tile = rows // 4
+    z, y = me // 2, me % 2
+    side = z // 2
+    inner = (z + side) % 2
+    at_z = {"a": 3 * side, "c": 1 + side, "g": 3 - 3 * side, "e": 2 - side}
+    row = {k: 2 * v + y for k, v in at_z.items()}
+    row.update({OVER_Y[k]: 2 * v + 1 - y for k, v in at_z.items()})
+
+    loads = [
+        pltpu.make_async_copy(
+            feat_hbm.at[pl.ds(i * tile, tile)], feat.at[pl.ds(i * tile, tile)], lsem.at[i]
+        )
+        for i in range(4)
+    ]
+    loads.append(pltpu.make_async_copy(res_hbm, res, lsem.at[4]))
+    loads.append(pltpu.make_async_copy(inv_hbm, inv, lsem.at[5]))
+    for load in loads:
+        load.start()
+    barrier = pltpu.get_barrier_semaphore()
+    z_near = 4 * side + 1 - z
+    for target in ({"row": 2 * z + 1 - y}, {"row": 2 * z_near + y}, {"col": 1 - core}):
+        pl.semaphore_signal(barrier, inc=1, device_id=target, device_id_type=MESH)
+
+    @pl.when(inner == 1)
+    def _():
+        pl.semaphore_signal(barrier, inc=1, device_id={"row": row["e"]}, device_id_type=MESH)
+
+    def message(item, link, target):
+        r = row[item[1]]
+        if item[0] == "X":
+            p = int(item[2])
+            ref = xall.at[r, pl.ds(p * quarter, quarter)]
+            src, dst, send, recv = ref, ref, xs.at[link, r, p], xr.at[r, p]
+        elif item[0] == "C":
+            src, dst, send, recv = call.at[r], call.at[r], cs.at[link, r], cr.at[r]
+        elif item[0] == "R":
+            src, dst, send, recv = own.at[r], part.at[r], rs.at[r], rr.at[r]
+        elif item[0] == "S":
+            src, dst, send, recv = part.at[r], half_sum.at[r], ss.at[r], sr.at[r]
+        else:
+            src, dst, send, recv = own.at[r], col_sum.at[r], ts.at[r], tr.at[r]
+        return pltpu.make_async_remote_copy(
+            src_ref=src, dst_ref=dst, send_sem=send, recv_sem=recv, device_id={"row": row[target]},
+            device_id_type=MESH,
+        )
+
+    base = me * rows
+
+    def local(i):
+        return jnp.maximum(jnp.minimum(ids[i] - base, rows - 1), 0)
+
+    def gather_x(p):
+        def body(i, _):
+            i = p * quarter + i
+            xall[me, pl.ds(i, 1), :] = feat[pl.ds(local(core * half + i), 1), :]
+            return 0
+
+        lax.fori_loop(0, quarter, body, 0, unroll=8)
+
+    def gather_res():
+        def body(i, _):
+            change[pl.ds(i, 1), :] = res[pl.ds(local(i), 1), :]
+            return 0
+
+        lax.fori_loop(0, blk, body, 0, unroll=8)
+        hi, lo = split(change[pl.ds(0, blk)])
+        bres[0] = hi
+        bres[1] = lo
+
+    def partial_value(k):
+        own[row[k]] = dot3(split(inv[row[k], 0]), (bres[0], bres[1]), NN)
+
+    def split_feat():
+        def body(i, _):
+            at = pl.ds(pl.multiple_of(i * half, half), half)
+            hi, lo = split(feat[at])
+            fhi[at] = hi
+            flo[at] = lo
+            return 0
+
+        lax.fori_loop(0, rows // half, body, 0)
+
+    def load_x(chunks):
+        for j, k in enumerate(chunks):
+            hi, lo = split(xall[row[k]])
+            xh[pl.ds(j * half, half)] = hi
+            xl[pl.ds(j * half, half)] = lo
+
+    def gram(slot, chunks, first, last):
+        cols = len(chunks) * half
+        to = pl.ds(slot * half, cols)
+
+        def body(i, _):
+            at = pl.ds(pl.multiple_of(i * tile, tile), tile)
+            g = dot3((fhi[at], flo[at]), (xh[pl.ds(0, cols)], xl[pl.ds(0, cols)]), NT)
+            g = g * (1.0 / feats) + 0.5
+            hi, lo = split(g * g)
+            khi[at, to] = hi
+            klo[at, to] = lo
+            return 0
+
+        lax.fori_loop(first, last, body, 0)
+
+    def load_c(chunks):
+        for j, k in enumerate(chunks):
+            hi, lo = split(call[row[k]])
+            chi[pl.ds(j * half, half)] = hi
+            clo[pl.ds(j * half, half)] = lo
+
+    def product(slot, at):
+        to = pl.ds(slot * half, blk)
+        return dot3((khi[at, to], klo[at, to]), (chi[...], clo[...]), NN)
+
+    def apply(slot, chunks, first):
+        load_c(chunks)
+
+        def body(i, _):
+            at = pl.ds(pl.multiple_of(i * tile, tile), tile)
+            add = product(slot, at)
+            change[at] = add if first else change[at] + add
+            return 0
+
+        lax.fori_loop(0, 4, body, 0)
+
+    mine = pl.ds(pl.multiple_of(core * width, width), width)
+    theirs = pl.ds(pl.multiple_of((1 - core) * width, width), width)
+
+    def swap(i):
+        at = pl.ds(i * tile, tile)
+        return pltpu.make_async_remote_copy(
+            src_ref=change.at[at, theirs], dst_ref=ebuf.at[at], send_sem=es.at[i],
+            recv_sem=er.at[i], device_id={"col": 1 - core}, device_id_type=MESH,
+        )
+
+    def finish(slot, chunks):
+        load_c(chunks)
+        for i in range(4):
+            at = pl.ds(i * tile, tile)
+            change[at] += product(slot, at)
+            swap(i).start()
+        for i in range(4):
+            at = pl.ds(i * tile, tile)
+            swap(i).wait_recv()
+            out[at] = res[at, mine] - (change[at, mine] + ebuf[at])
+
+    def run(is_inner, here, sends, arrivals, steps):
+        queues = [[link, target, list(order)] for link, target, order in sends]
+        have, sent = set(), []
+
+        def issue():
+            for link, target, order in queues:
+                while order and order[0] in have:
+                    item = order.pop(0)
+                    copy = message(item, link, target)
+                    copy.start()
+                    sent.append(copy)
+
+        for load in loads[:4]:
+            load.wait()
+        for p in range(4):
+            gather_x(p)
+            have.add(f"X{here}{p}")
+            if p == 0:
+                pl.semaphore_wait(barrier, 4 if is_inner else 3)
+            issue()
+        loads[4].wait()
+        loads[5].wait()
+        gather_res()
+        for k in "fdhbgeac":
+            partial_value(k)
+            if not is_inner:
+                have.add("R" + k)
+                issue()
+        split_feat()
+        load_x(here)
+        gram(*steps[0])
+
+        def sums():
+            for k in "efgh":
+                if "S" + k not in have and "R" + k in have:
+                    r = row[k]
+                    part[r] = part[r] + own[r]
+                    have.add("S" + k)
+            for k in "bd":
+                if "T" + k not in have and {"R" + k, "s" + k} <= have:
+                    r = row[k]
+                    own[r] = own[r] + part[r] + half_sum[r]
+                    have.add("T" + k)
+            for k in "ac":
+                if "C" + k not in have and {"R" + k, "s" + k, "t" + k} <= have:
+                    r = row[k]
+                    call[r] = own[r] + part[r] + half_sum[r] + col_sum[r]
+                    have.add("C" + k)
+
+        for at, group in enumerate(arrivals):
+            for item in group:
+                message(item, 0, OVER_Y[here]).wait_recv()
+                have.add(item if item[0] not in "ST" else item.lower())
+                if is_inner:
+                    sums()
+                issue()
+            for step in steps[1].get(at + 1, ()):
+                step()
+        assert not any(order for _, _, order in queues)
+        for copy in sent:
+            copy.wait_send()
+        for i in range(4):
+            swap(i).wait_send()
+
+    def do(f, *args):
+        return functools.partial(f, *args)
+
+    @pl.when(inner == 0)
+    def _():
+        run(
+            False, "a",
+            ((1, "c", CORNER_Z), (0, "b", CORNER_Y)),
+            slots(seen(CORNER_Y, OVER_Y), INNER_Z),
+            (
+                (0, "a", 0, 4),
+                {
+                    4: [do(load_x, "cb"), do(gram, 1, "cb", 0, 2)],
+                    5: [do(gram, 1, "cb", 2, 4)],
+                    9: [do(load_x, "ed"), do(gram, 5, "ed", 0, 2)],
+                    10: [do(gram, 5, "ed", 2, 4)],
+                    14: [do(load_x, "hg"), do(gram, 3, "hg", 0, 2)],
+                    15: [do(gram, 3, "hg", 2, 4), do(apply, 0, "ac", True)],
+                    16: [do(load_x, "f"), do(gram, 7, "f", 0, 4), do(apply, 4, "ge", False)],
+                    17: [do(apply, 2, "bh", False)],
+                    18: [do(finish, 6, "df")],
+                },
+            ),
+        )
+
+    @pl.when(inner == 1)
+    def _():
+        run(
+            True, "c",
+            ((1, "a", INNER_Z), (2, "e", INNER_W), (0, "d", INNER_Y)),
+            slots(CORNER_Z, seen(INNER_W, OVER_Z), seen(INNER_Y, OVER_Y)),
+            (
+                (0, "c", 0, 4),
+                {
+                    6: [do(load_x, "ed"), do(gram, 6, "ed", 0, 2)],
+                    7: [do(gram, 6, "ed", 2, 4)],
+                    10: [do(load_x, "ag"), do(gram, 1, "ag", 0, 2)],
+                    11: [do(gram, 1, "ag", 2, 4)],
+                    12: [do(load_x, "h"), do(gram, 5, "h", 0, 4)],
+                    13: [do(apply, 0, "ca", True)],
+                    14: [do(apply, 6, "ed", False)],
+                    16: [do(load_x, "bf"), do(gram, 3, "bf", 0, 4)],
+                    17: [do(apply, 2, "gb", False)],
+                    18: [do(finish, 4, "fh")],
+                },
+            ),
+        )
+
+
+def on_mesh(inverse, features, residual, block_ids):
+    n, cores = lax.axis_size("row"), lax.axis_size("col")
+    rows, feats = features.shape
+    rhs = residual.shape[1]
+    blk = block_ids.shape[0]
+    half, tile = blk // cores, rows // 4
+    any_spec = pl.BlockSpec(memory_space=pl.ANY)
+    dma = pltpu.SemaphoreType.DMA
+    return pl.pallas_call(
+        mesh_kernel,
+        out_shape=jax.ShapeDtypeStruct((rows, rhs // cores), F32),
+        in_specs=[pl.BlockSpec(memory_space=pltpu.SMEM), any_spec, any_spec, any_spec],
+        out_specs=pl.BlockSpec(memory_space=pltpu.VMEM),
+        scratch_shapes=[
+            pltpu.VMEM((rows, feats), F32),
+            pltpu.VMEM((rows, feats), BF16),
+            pltpu.VMEM((rows, feats), BF16),
+            pltpu.VMEM((rows, rhs), F32),
+            pltpu.VMEM(inverse.shape, F32),
+            pltpu.VMEM((2, blk, rhs), BF16),
+            pltpu.VMEM((n, half, feats), F32),
+            pltpu.VMEM((blk, feats), BF16),
+            pltpu.VMEM((blk, feats), BF16),
+            pltpu.VMEM((rows, n * half), BF16),
+            pltpu.VMEM((rows, n * half), BF16),
+            pltpu.VMEM((n, half, rhs), F32),
+            pltpu.VMEM((blk, rhs), BF16),
+            pltpu.VMEM((blk, rhs), BF16),
+            pltpu.VMEM((n, half, rhs), F32),
+            pltpu.VMEM((n, half, rhs), F32),
+            pltpu.VMEM((n, half, rhs), F32),
+            pltpu.VMEM((n, half, rhs), F32),
+            pltpu.VMEM((rows, rhs), F32),
+            pltpu.VMEM((rows, rhs // cores), F32),
+            dma((6,)),
+            dma((3, n, 4)),
+            dma((n, 4)),
+            dma((3, n)),
+            dma((n,)),
+            dma((n,)),
+            dma((n,)),
+            dma((n,)),
+            dma((n,)),
+            dma((n,)),
+            dma((n,)),
+            dma((4,)),
+            dma((4,)),
+        ],
+        compiler_params=pltpu.CompilerParams(
+            collective_id=0, has_side_effects=True, vmem_limit_bytes=67043328
+        ),
+    )(block_ids, features, residual, inverse)
+
+
 def two_lines(mesh):
     line = mesh.devices
     line = line[0, :, 0] if line.ndim == 3 else line.ravel()
@@ -286,8 +641,12 @@
 
 
 def solution(mesh):
+    snake = two_lines(mesh)
+    on_device = functools.partial(ring, snake)
+    if snake and mesh.shape["row"] == len(OVER_Y):
+        on_device = on_mesh
     return jax.shard_map(
-        functools.partial(on_device, two_lines(mesh)),
+        on_device,
         mesh=mesh,
         in_specs=(
             P("groups", "col", None, "row"),

time: 77.4 us -> 65.4 us (0.84)
  Pallas kernels: 75.3 us -> 63.3 us
    pallas_call x1, Pallas kernels: 75.3 us -> 63.3 us  [on_mesh(): pl.pallas_call(mesh_kernel, out_shape=jax.ShapeDtypeStruct((rows, rhs //...]
where the time goes in v1:
time: 65.4 us; the launch traced here: 65.2 us
  Pallas kernels  63.3 us (97%)
  local copies, waits for them, and re-layouts  1.87 us (3%)
    pallas_call x1, Pallas kernels, on_mesh(): pl.pallas_call(mesh_kernel, out_shape=jax.ShapeDtypeStruct((rows, rhs //...  63.3 us
    unnamed x1, local copies, waits for them, and re-layouts  1.87 us

profile of v1, /device:TPU:1, one launch (start us, length us, event | category | flops | bytes accessed | tf_op | source)
XLA Modules:
  0.0 65.2 jit_solution(5100444089076125444)
XLA Ops:
  0.0 63.3 %shard_map.46 = f32[1024,128]{1,0:T(8,128)} custom-call(s32[256]{0:T(256)} %ids.1, f32[1024,1024]{1,0:T(8,128)} %feat_hbm.1, f32[1024,256]{1,0:T(8,128)} %res_hbm.1, f32[8,1,128,256]{3,2,1,0:T(8,128)} %inv_hbm.1), custom_call_target="tpu_custom_call" | custom-call | tf_op jit(solution)/shard_map/pallas_call | solution.py:588
  63.3 1.9 %copy.6 = f32[1024,128]{1,0:T(8,128)} copy(f32[1024,128]{1,0:T(8,128)} %shard_map.46) | data formatting | bytes 1048576

commit v2 on v1

--- a/solution.py
+++ b/solution.py
@@ -309,8 +309,8 @@
 
 
 def mesh_kernel(
-    ids, feat_hbm, res_hbm, inv_hbm, out, feat, fhi, flo, res, inv, bres, xall, xh, xl, khi, klo,
-    call, chi, clo, own, part, half_sum, col_sum, change, ebuf, lsem, xs, xr, cs, cr, rs, rr, ss,
+    ids_hbm, feat_hbm, res_hbm, inv_hbm, out, ids, feat, fhi, flo, res, inv, bres, xall, xh, xl,
+    khi, klo, call, chi, clo, own, part, half_sum, col_sum, change, ebuf, lsem, xs, xr, cs, cr, rs, rr, ss,
     sr, ts, tr, es, er,
 ):
     me, core = lax.axis_index("row"), lax.axis_index("col")
@@ -333,6 +333,7 @@
         )
         for i in range(4)
     ]
+    loads.append(pltpu.make_async_copy(ids_hbm, ids, lsem.at[6]))
     loads.append(pltpu.make_async_copy(res_hbm, res, lsem.at[4]))
     loads.append(pltpu.make_async_copy(inv_hbm, inv, lsem.at[5]))
     for load in loads:
@@ -476,7 +477,7 @@
                     copy.start()
                     sent.append(copy)
 
-        for load in loads[:4]:
+        for load in loads[:5]:
             load.wait()
         for p in range(4):
             gather_x(p)
@@ -484,8 +485,8 @@
             if p == 0:
                 pl.semaphore_wait(barrier, 4 if is_inner else 3)
             issue()
-        loads[4].wait()
         loads[5].wait()
+        loads[6].wait()
         gather_res()
         for k in "fdhbgeac":
             partial_value(k)
@@ -583,14 +584,19 @@
     rhs = residual.shape[1]
     blk = block_ids.shape[0]
     half, tile = blk // cores, rows // 4
-    any_spec = pl.BlockSpec(memory_space=pl.ANY)
+    hbm_spec = pl.BlockSpec(memory_space=pltpu.HBM)
     dma = pltpu.SemaphoreType.DMA
+    args = [
+        pltpu.with_memory_space_constraint(v, pltpu.HBM)
+        for v in (block_ids, features, residual, inverse)
+    ]
     return pl.pallas_call(
         mesh_kernel,
         out_shape=jax.ShapeDtypeStruct((rows, rhs // cores), F32),
-        in_specs=[pl.BlockSpec(memory_space=pltpu.SMEM), any_spec, any_spec, any_spec],
+        in_specs=[hbm_spec] * 4,
         out_specs=pl.BlockSpec(memory_space=pltpu.VMEM),
         scratch_shapes=[
+            pltpu.SMEM(block_ids.shape, jnp.int32),
             pltpu.VMEM((rows, feats), F32),
             pltpu.VMEM((rows, feats), BF16),
             pltpu.VMEM((rows, feats), BF16),
@@ -611,7 +617,7 @@
             pltpu.VMEM((n, half, rhs), F32),
             pltpu.VMEM((rows, rhs), F32),
             pltpu.VMEM((rows, rhs // cores), F32),
-            dma((6,)),
+            dma((7,)),
             dma((3, n, 4)),
             dma((n, 4)),
             dma((3, n)),
@@ -626,9 +632,9 @@
             dma((4,)),
         ],
         compiler_params=pltpu.CompilerParams(
-            collective_id=0, has_side_effects=True, vmem_limit_bytes=67043328
+            collective_id=0, has_side_effects=True, vmem_limit_bytes=34 * 2**20
         ),
-    )(block_ids, features, residual, inverse)
+    )(*args)
 
 
 def two_lines(mesh):

time: 65.4 us -> 62.8 us (0.960)
  Pallas kernels: 63.3 us -> 61.9 us
  local copies, waits for them, and re-layouts: 1.87 us -> 0.8 us
    pallas_call x1, Pallas kernels: 63.3 us -> 61.9 us  [on_mesh(): pl.pallas_call(mesh_kernel, out_shape=jax.ShapeDtypeStruct((rows, rhs //...]
    unnamed x1, local copies, waits for them, and re-layouts: 1.87 us -> 0.8 us
where the time goes in v2:
time: 62.8 us; the launch traced here: 62.7 us
  Pallas kernels  61.9 us (99%)
  local copies, waits for them, and re-layouts  0.8 us (1%)
    pallas_call x1, Pallas kernels, on_mesh(): pl.pallas_call(mesh_kernel, out_shape=jax.ShapeDtypeStruct((rows, rhs //...  61.9 us

profile of v2, /device:TPU:1, one launch (start us, length us, event | category | flops | bytes accessed | tf_op | source)
XLA Modules:
  0.0 62.7 jit_solution(13236141715108289856)
XLA Ops:
  0.0 61.9 %shard_map.46 = f32[1024,128]{1,0:T(8,128)S(1)} custom-call(s32[256]{0:T(256)} %ids_hbm.1, f32[1024,1024]{1,0:T(8,128)} %feat_hbm.1, f32[1024,256]{1,0:T(8,128)} %res_hbm.1, f32[8,1,128,256]{3,2,1,0:T(8,128)} %inv_hbm.1), custom_call_target="tpu_custom_call" | custom-call | tf_op jit(solution)/shard_map/pallas_call | solution.py:593
  61.9 0.8 %copy.6 = f32[1024,128]{1,0:T(8,128)} copy(f32[1024,128]{1,0:T(8,128)S(1)} %shard_map.46) | data formatting | bytes 1048576

commit v3 on v2

--- a/solution.py
+++ b/solution.py
@@ -281,8 +281,8 @@
     "Xb0", "Xb1", "Xb2", "Xb3",
 )
 CORNER_Y = (
-    "Xa0", "Xa2", "Xa3", "Xa1", "Xc0", "Xc1", "Xc2", "Xc3", "Xe0", "Xg0", "Xe1", "Xg1",
-    "Xg2", "Xg3", "Xe2", "Xe3", "Cg", "Ce",
+    "Xa0", "Xa2", "Xa3", "Xa1", "Xc0", "Xc1", "Xc2", "Xc3", "Xe2", "Xe3", "Xe0", "Xe1",
+    "Xg0", "Xg1", "Xg2", "Xg3", "Cg", "Ce",
 )
 INNER_Z = (
     "Xc0", "Xc1", "Xc2", "Xc3", "Xe2", "Xe3", "Xe0", "Xg0", "Xe1", "Xg1", "Xg2", "Xg3",
@@ -336,7 +336,8 @@
     loads.append(pltpu.make_async_copy(ids_hbm, ids, lsem.at[6]))
     loads.append(pltpu.make_async_copy(res_hbm, res, lsem.at[4]))
     loads.append(pltpu.make_async_copy(inv_hbm, inv, lsem.at[5]))
-    for load in loads:
+    loads[4].start()
+    for load in loads[:4] + loads[5:]:
         load.start()
     barrier = pltpu.get_barrier_semaphore()
     z_near = 4 * side + 1 - z
@@ -408,17 +409,18 @@
             xh[pl.ds(j * half, half)] = hi
             xl[pl.ds(j * half, half)] = lo
 
-    def gram(slot, chunks, first, last):
+    def gram(to, chunks, first, last):
         cols = len(chunks) * half
-        to = pl.ds(slot * half, cols)
 
         def body(i, _):
             at = pl.ds(pl.multiple_of(i * tile, tile), tile)
             g = dot3((fhi[at], flo[at]), (xh[pl.ds(0, cols)], xl[pl.ds(0, cols)]), NT)
             g = g * (1.0 / feats) + 0.5
             hi, lo = split(g * g)
-            khi[at, to] = hi
-            klo[at, to] = lo
+            for j, slot in enumerate(to):
+                cut = slice(j * half, (j + 1) * half)
+                khi[at, pl.ds(slot * half, half)] = hi[:, cut]
+                klo[at, pl.ds(slot * half, half)] = lo[:, cut]
             return 0
 
         lax.fori_loop(first, last, body, 0)
@@ -447,8 +449,10 @@
     mine = pl.ds(pl.multiple_of(core * width, width), width)
     theirs = pl.ds(pl.multiple_of((1 - core) * width, width), width)
 
+    piece = rows // 1
+
     def swap(i):
-        at = pl.ds(i * tile, tile)
+        at = pl.ds(i * piece, piece)
         return pltpu.make_async_remote_copy(
             src_ref=change.at[at, theirs], dst_ref=ebuf.at[at], send_sem=es.at[i],
             recv_sem=er.at[i], device_id={"col": 1 - core}, device_id_type=MESH,
@@ -456,12 +460,12 @@
 
     def finish(slot, chunks):
         load_c(chunks)
-        for i in range(4):
-            at = pl.ds(i * tile, tile)
+        for i in range(1):
+            at = pl.ds(i * piece, piece)
             change[at] += product(slot, at)
             swap(i).start()
-        for i in range(4):
-            at = pl.ds(i * tile, tile)
+        for i in range(1):
+            at = pl.ds(i * piece, piece)
             swap(i).wait_recv()
             out[at] = res[at, mine] - (change[at, mine] + ebuf[at])
 
@@ -526,7 +530,7 @@
         assert not any(order for _, _, order in queues)
         for copy in sent:
             copy.wait_send()
-        for i in range(4):
+        for i in range(1):
             swap(i).wait_send()
 
     def do(f, *args):
@@ -539,16 +543,17 @@
             ((1, "c", CORNER_Z), (0, "b", CORNER_Y)),
             slots(seen(CORNER_Y, OVER_Y), INNER_Z),
             (
-                (0, "a", 0, 4),
+                ((0,), "a", 0, 4),
                 {
-                    4: [do(load_x, "cb"), do(gram, 1, "cb", 0, 2)],
-                    5: [do(gram, 1, "cb", 2, 4)],
-                    9: [do(load_x, "ed"), do(gram, 5, "ed", 0, 2)],
-                    10: [do(gram, 5, "ed", 2, 4)],
-                    14: [do(load_x, "hg"), do(gram, 3, "hg", 0, 2)],
-                    15: [do(gram, 3, "hg", 2, 4), do(apply, 0, "ac", True)],
-                    16: [do(load_x, "f"), do(gram, 7, "f", 0, 4), do(apply, 4, "ge", False)],
-                    17: [do(apply, 2, "bh", False)],
+                    4: [do(load_x, "cb"), do(gram, (1, 4), "cb", 0, 2)],
+                    5: [do(gram, (1, 4), "cb", 2, 4)],
+                    9: [do(load_x, "ed"), do(gram, (3, 6), "ed", 0, 2)],
+                    10: [do(gram, (3, 6), "ed", 2, 4)],
+                    12: [do(load_x, "gf"), do(gram, (2, 7), "gf", 0, 2)],
+                    13: [do(gram, (2, 7), "gf", 2, 4)],
+                    14: [do(apply, 0, "ac", True)],
+                    16: [do(load_x, "h"), do(gram, (5,), "h", 0, 4), do(apply, 2, "ge", False)],
+                    17: [do(apply, 4, "bh", False)],
                     18: [do(finish, 6, "df")],
                 },
             ),
@@ -561,18 +566,18 @@
             ((1, "a", INNER_Z), (2, "e", INNER_W), (0, "d", INNER_Y)),
             slots(CORNER_Z, seen(INNER_W, OVER_Z), seen(INNER_Y, OVER_Y)),
             (
-                (0, "c", 0, 4),
+                ((0,), "c", 0, 4),
                 {
-                    6: [do(load_x, "ed"), do(gram, 6, "ed", 0, 2)],
-                    7: [do(gram, 6, "ed", 2, 4)],
-                    10: [do(load_x, "ag"), do(gram, 1, "ag", 0, 2)],
-                    11: [do(gram, 1, "ag", 2, 4)],
-                    12: [do(load_x, "h"), do(gram, 5, "h", 0, 4)],
+                    6: [do(load_x, "ed"), do(gram, (4, 5), "ed", 0, 2)],
+                    7: [do(gram, (4, 5), "ed", 2, 4)],
+                    10: [do(load_x, "ag"), do(gram, (1, 7), "ag", 0, 2)],
+                    11: [do(gram, (1, 7), "ag", 2, 4)],
+                    12: [do(load_x, "h"), do(gram, (2,), "h", 0, 4)],
                     13: [do(apply, 0, "ca", True)],
-                    14: [do(apply, 6, "ed", False)],
-                    16: [do(load_x, "bf"), do(gram, 3, "bf", 0, 4)],
-                    17: [do(apply, 2, "gb", False)],
-                    18: [do(finish, 4, "fh")],
+                    14: [do(apply, 4, "ed", False)],
+                    16: [do(load_x, "bf"), do(gram, (6, 3), "bf", 0, 4)],
+                    17: [do(apply, 6, "bg", False)],
+                    18: [do(finish, 2, "hf")],
                 },
             ),
         )
@@ -628,8 +633,8 @@
             dma((n,)),
             dma((n,)),
             dma((n,)),
-            dma((4,)),
-            dma((4,)),
+            dma((1,)),
+            dma((1,)),
         ],
         compiler_params=pltpu.CompilerParams(
             collective_id=0, has_side_effects=True, vmem_limit_bytes=34 * 2**20

time: 62.8 us -> 62.4 us (level)
  no operation moved by 1% of the time
where the time goes in v3:
time: 62.4 us; the launch traced here: 62.3 us
  Pallas kernels  61.4 us (98%)
  local copies, waits for them, and re-layouts  0.8 us (1%)
    pallas_call x1, Pallas kernels, on_mesh(): pl.pallas_call(mesh_kernel, out_shape=jax.ShapeDtypeStruct((rows, rhs //...  61.4 us

profile of v3, /device:TPU:1, one launch (start us, length us, event | category | flops | bytes accessed | tf_op | source)
XLA Modules:
  0.0 62.3 jit_solution(16007523280358102753)
XLA Ops:
  0.0 61.4 %shard_map.46 = f32[1024,128]{1,0:T(8,128)S(1)} custom-call(s32[256]{0:T(256)} %ids_hbm.1, f32[1024,1024]{1,0:T(8,128)} %feat_hbm.1, f32[1024,256]{1,0:T(8,128)} %res_hbm.1, f32[8,1,128,256]{3,2,1,0:T(8,128)} %inv_hbm.1), custom_call_target="tpu_custom_call" | custom-call | tf_op jit(solution)/shard_map/pallas_call | solution.py:598
  61.5 0.8 %copy.6 = f32[1024,128]{1,0:T(8,128)} copy(f32[1024,128]{1,0:T(8,128)S(1)} %shard_map.46) | data formatting | bytes 1048576

commit v4 on v3

--- a/solution.py
+++ b/solution.py
@@ -309,17 +309,18 @@
 
 
 def mesh_kernel(
-    ids_hbm, feat_hbm, res_hbm, inv_hbm, out, ids, feat, fhi, flo, res, inv, bres, xall, xh, xl,
+    ids_hbm, feat_hbm, res_hbm, inv_hbm, out, ids, feat0, feat1, feat2, feat3, fhi, flo, res, inv, bres, xall, xh, xl,
     khi, klo, call, chi, clo, own, part, half_sum, col_sum, change, ebuf, lsem, xs, xr, cs, cr, rs, rr, ss,
     sr, ts, tr, es, er,
 ):
     me, core = lax.axis_index("row"), lax.axis_index("col")
-    rows, feats = feat.shape
+    feat = (feat0, feat1, feat2, feat3)
+    rows, feats = fhi.shape
     blk = ids.shape[0]
     half = blk // 2
     quarter = half // 4
     width = out.shape[1]
-    tile = rows // 4
+    tile, strip = rows // 4, feats // 4
     z, y = me // 2, me % 2
     side = z // 2
     inner = (z + side) % 2
@@ -329,16 +330,16 @@
 
     loads = [
         pltpu.make_async_copy(
-            feat_hbm.at[pl.ds(i * tile, tile)], feat.at[pl.ds(i * tile, tile)], lsem.at[i]
+            feat_hbm.at[pl.ds(0, rows), pl.ds(i * strip, strip)],
+            feat[i], lsem.at[i],
         )
         for i in range(4)
     ]
     loads.append(pltpu.make_async_copy(ids_hbm, ids, lsem.at[6]))
     loads.append(pltpu.make_async_copy(res_hbm, res, lsem.at[4]))
     loads.append(pltpu.make_async_copy(inv_hbm, inv, lsem.at[5]))
-    loads[4].start()
-    for load in loads[:4] + loads[5:]:
-        load.start()
+    for i in (4, 0, 1):
+        loads[i].start()
     barrier = pltpu.get_barrier_semaphore()
     z_near = 4 * side + 1 - z
     for target in ({"row": 2 * z + 1 - y}, {"row": 2 * z_near + y}, {"col": 1 - core}):
@@ -348,11 +349,13 @@
     def _():
         pl.semaphore_signal(barrier, inc=1, device_id={"row": row["e"]}, device_id_type=MESH)
 
-    def message(item, link, target):
+    def message(item, link, target, q=None):
         r = row[item[1]]
         if item[0] == "X":
             p = int(item[2])
-            ref = xall.at[r, pl.ds(p * quarter, quarter)]
+            ref, p = xall.at[r, pl.ds(p * quarter, quarter)], p + 3
+            if q is not None:
+                ref, p = xall.at[r, pl.ds(0, quarter), pl.ds(q * strip, strip)], q
             src, dst, send, recv = ref, ref, xs.at[link, r, p], xr.at[r, p]
         elif item[0] == "C":
             src, dst, send, recv = call.at[r], call.at[r], cs.at[link, r], cr.at[r]
@@ -372,10 +375,16 @@
     def local(i):
         return jnp.maximum(jnp.minimum(ids[i] - base, rows - 1), 0)
 
-    def gather_x(p):
+    def copies(item, link, target):
+        pieces = range(4) if item[0] == "X" and item[2] == "0" else (None,)
+        return [message(item, link, target, q) for q in pieces]
+
+    def gather_x(p, strips):
         def body(i, _):
             i = p * quarter + i
-            xall[me, pl.ds(i, 1), :] = feat[pl.ds(local(core * half + i), 1), :]
+            for q in strips:
+                v = feat[q][pl.ds(local(core * half + i), 1), :]
+                xall[me, pl.ds(i, 1), pl.ds(q * strip, strip)] = v
             return 0
 
         lax.fori_loop(0, quarter, body, 0, unroll=8)
@@ -396,9 +405,10 @@
     def split_feat():
         def body(i, _):
             at = pl.ds(pl.multiple_of(i * half, half), half)
-            hi, lo = split(feat[at])
-            fhi[at] = hi
-            flo[at] = lo
+            for q in range(4):
+                hi, lo = split(feat[q][at])
+                fhi[at, pl.ds(q * strip, strip)] = hi
+                flo[at, pl.ds(q * strip, strip)] = lo
             return 0
 
         lax.fori_loop(0, rows // half, body, 0)
@@ -477,17 +487,27 @@
             for link, target, order in queues:
                 while order and order[0] in have:
                     item = order.pop(0)
-                    copy = message(item, link, target)
-                    copy.start()
-                    sent.append(copy)
-
-        for load in loads[:5]:
-            load.wait()
-        for p in range(4):
-            gather_x(p)
+                    for copy in copies(item, link, target):
+                        copy.start()
+                        sent.append(copy)
+
+        loads[4].wait()
+        for q in range(4):
+            loads[q].wait()
+            for i in {0: (2, 3), 1: (5, 6)}.get(q, ()):
+                loads[i].start()
+            gather_x(0, (q,))
+            if q == 0:
+                pl.semaphore_wait(barrier, 4 if is_inner else 3)
+            for link, target, _ in queues:
+                sent.append(message(f"X{here}0", link, target, q))
+                sent[-1].start()
+        for _, _, order in queues:
+            assert order.pop(0) == f"X{here}0"
+        have.add(f"X{here}0")
+        for p in range(1, 4):
+            gather_x(p, range(4))
             have.add(f"X{here}{p}")
-            if p == 0:
-                pl.semaphore_wait(barrier, 4 if is_inner else 3)
             issue()
         loads[5].wait()
         loads[6].wait()
@@ -520,7 +540,8 @@
 
         for at, group in enumerate(arrivals):
             for item in group:
-                message(item, 0, OVER_Y[here]).wait_recv()
+                for copy in copies(item, 0, OVER_Y[here]):
+                    copy.wait_recv()
                 have.add(item if item[0] not in "ST" else item.lower())
                 if is_inner:
                     sums()
@@ -602,7 +623,10 @@
         out_specs=pl.BlockSpec(memory_space=pltpu.VMEM),
         scratch_shapes=[
             pltpu.SMEM(block_ids.shape, jnp.int32),
-            pltpu.VMEM((rows, feats), F32),
+            pltpu.VMEM((rows, feats // 4), F32),
+            pltpu.VMEM((rows, feats // 4), F32),
+            pltpu.VMEM((rows, feats // 4), F32),
+            pltpu.VMEM((rows, feats // 4), F32),
             pltpu.VMEM((rows, feats), BF16),
             pltpu.VMEM((rows, feats), BF16),
             pltpu.VMEM((rows, rhs), F32),
@@ -623,8 +647,8 @@
             pltpu.VMEM((rows, rhs), F32),
             pltpu.VMEM((rows, rhs // cores), F32),
             dma((7,)),
-            dma((3, n, 4)),
-            dma((n, 4)),
+            dma((3, n, 7)),
+            dma((n, 7)),
             dma((3, n)),
             dma((n,)),
             dma((n,)),

time: 62.4 us -> 62.2 us (level)
  no operation moved by 1% of the time
where the time goes in v4:
time: 62.2 us; the launch traced here: 62 us
  Pallas kernels  61.2 us (98%)
  local copies, waits for them, and re-layouts  0.8 us (1%)
    pallas_call x1, Pallas kernels, on_mesh(): pl.pallas_call(mesh_kernel, out_shape=jax.ShapeDtypeStruct((rows, rhs //...  61.2 us

profile of v4, /device:TPU:1, one launch (start us, length us, event | category | flops | bytes accessed | tf_op | source)
XLA Modules:
  0.0 62.0 jit_solution(325567408993283889)
XLA Ops:
  0.0 61.2 %shard_map.46 = f32[1024,128]{1,0:T(8,128)S(1)} custom-call(s32[256]{0:T(256)} %ids_hbm.1, f32[1024,1024]{1,0:T(8,128)} %feat_hbm.1, f32[1024,256]{1,0:T(8,128)} %res_hbm.1, f32[8,1,128,256]{3,2,1,0:T(8,128)} %inv_hbm.1), custom_call_target="tpu_custom_call" | custom-call | tf_op jit(solution)/shard_map/pallas_call | solution.py:619
  61.2 0.8 %copy.6 = f32[1024,128]{1,0:T(8,128)} copy(f32[1024,128]{1,0:T(8,128)S(1)} %shard_map.46) | data formatting | bytes 1048576
